TPU v7x, 32 devices: a whole 2x2x4 slice. The times are simulated.
32 devices in a mesh: ctx: 8 (over z, x), tp: 4 (over y, core).
Axes of the slice: x: 2, y: 2, z: 4, core: 2. Of those that a mesh axis runs over, the one named last changes fastest.
Arguments:
- queries: bfloat16 [64, 4, 64, 128], P('ctx', None, 'tp'), may hold values from -250 to 250
- new_keys: bfloat16 [64, 4, 8, 128], P('ctx', None, 'tp'), may hold values from -6 to 6
- new_values: bfloat16 [64, 4, 8, 128], P('ctx', None, 'tp'), may hold values from -24 to 24
- key_pool: bfloat16 [512, 256, 8, 128], P('ctx', None, 'tp'), may hold values from -6 to 6
- value_pool: bfloat16 [512, 256, 8, 128], P('ctx', None, 'tp'), may hold values from -24 to 24
- slot_block: int32 [512], P('ctx'), may hold values from -1 to 8191, as said below
- lengths: int32 [64], replicated, may hold values from 1 to 32768, as said below
- out_weight: bfloat16 [8192, 8192], P('tp', 'ctx'), may hold values from -0.0625 to 0.0625
Outputs:
- layer_out: bfloat16 [64, 4, 8192], P('tp', None, 'ctx')
Inputs may be any that keep to these rules, and one draw needn't show every extreme that they name: `slot_block`: each entry is r * 128 + j for block j of request r, or -1 for an empty slot. Every block j < b_r of every request r appears exactly once, where b_r = ceil(lengths[r] / 256). On each index of ctx the used slots come first. The owner of a request holds its first blocks as far as its slots reach; the remaining blocks lie on other indices of ctx. The blocks that one index of ctx holds of requests it does not own all belong to one request, and some index of ctx holds such blocks. `lengths`: some request has exactly 32768 positions.
All inputs are finite; a program needn't handle non-finite values.
Results may differ from a plain program's by a relative error of at most 0.006.
Values may be sent and summed in bfloat16 or wider, within the bound.
No kernel may reach another device: no remote copies, remote signals or barrier semaphores. Data moves between devices by JAX's collectives and lax.ppermute only.
A program may use at most 64 MiB of HBM per device.

v0:
```python
import jax
import jax.numpy as jnp
from jax import lax
from jax.sharding import PartitionSpec as P

MAXB = 128


def block_partial(decode_query_rows, gathered_keys, gathered_values, usable, pattern):
    head_width_size = decode_query_rows.shape[-1]
    logit_scores = jnp.einsum(
        pattern[0], decode_query_rows, gathered_keys, preferred_element_type=jnp.float32
    ) * head_width_size ** (-0.5)
    masked = jnp.where(usable, logit_scores, jnp.float32(-1e30))
    highest = jnp.max(masked, axis=-1)
    softmax_weights = jnp.where(
        usable, jnp.exp(masked - highest[..., None]), jnp.float32(0.0)
    ).astype(jnp.bfloat16)
    totals = jnp.sum(softmax_weights.astype(jnp.float32), axis=-1)
    weighted_sum = jnp.einsum(
        pattern[1], softmax_weights, gathered_values, preferred_element_type=jnp.float32
    )
    leading = highest.shape[0]
    return (
        highest.reshape(leading, -1),
        totals.reshape(leading, -1),
        weighted_sum.reshape(leading, -1, head_width_size),
    )


def finish(totals, weighted_sum, kv_heads, group_size, step_count):
    leading, row_width, head_width_size = weighted_sum.shape
    attention = (weighted_sum / totals[..., None]).reshape(
        leading, kv_heads, group_size, step_count, head_width_size
    )
    attention = attention.transpose(0, 3, 1, 2, 4).reshape(
        leading, step_count, kv_heads * group_size * head_width_size
    )
    return attention.astype(jnp.bfloat16)


def per_device(
    queries, new_keys, new_values, key_pool, value_pool, slot_block, lengths, out_weight
):
    owned_count, step_count, head_count, head_width_size = queries.shape
    kv_heads = new_keys.shape[2]
    group_size = head_count // kv_heads
    slot_count, block_len = (key_pool.shape[0], key_pool.shape[1])
    request_count = lengths.shape[0]
    every_query = lax.all_gather(queries, "ctx", axis=0, tiled=True)
    in_use = slot_block >= 0
    request = jnp.where(in_use, slot_block // MAXB, 0)
    position = (slot_block % MAXB * block_len)[:, None] + jnp.arange(block_len, dtype=jnp.int32)[
        None, :
    ]
    usable = in_use[:, None] & (position < lengths[request][:, None])
    picked = every_query[request].reshape(
        slot_count, step_count, kv_heads, group_size, head_width_size
    )
    slot_high, slot_total, slot_sum = block_partial(
        picked,
        key_pool,
        value_pool,
        usable[:, None, None, None, :],
        ("ptkgd,pbkd->pkgtb", "pkgtb,pbkd->pkgtd"),
    )
    own_queries = queries.reshape(owned_count, step_count, kv_heads, group_size, head_width_size)
    causal = jnp.arange(step_count)[:, None] >= jnp.arange(step_count)[None, :]
    own_high, own_total, own_sum = block_partial(
        own_queries,
        new_keys,
        new_values,
        causal[None, None, None],
        ("rtkgd,rskd->rkgts", "rkgts,rskd->rkgtd"),
    )
    member = (request[:, None] == jnp.arange(request_count, dtype=jnp.int32)[None, :]) & in_use[
        :, None
    ]
    req_high = jnp.max(
        jnp.where(member[:, :, None], slot_high[:, None, :], jnp.float32(-1e30)), axis=0
    )
    factor = jnp.exp(slot_high - req_high[request])
    member_f = member.astype(jnp.float32)
    req_total = jnp.dot(member_f.T, slot_total * factor, precision=lax.Precision.HIGHEST)
    req_sum = jnp.einsum(
        "pr,pqd->rqd", member_f, slot_sum * factor[..., None], precision=lax.Precision.HIGHEST
    )
    received = (
        lax.all_to_all(req_high, "ctx", split_axis=0, concat_axis=0, tiled=True),
        lax.all_to_all(req_total, "ctx", split_axis=0, concat_axis=0, tiled=True),
        lax.all_to_all(req_sum, "ctx", split_axis=0, concat_axis=0, tiled=True),
    )
    sources = lax.axis_size("ctx")
    row_width = req_high.shape[1]
    peaks = received[0].reshape(sources, owned_count, row_width)
    amounts = received[1].reshape(sources, owned_count, row_width)
    vectors = received[2].reshape(sources, owned_count, row_width, head_width_size)
    highest = jnp.maximum(jnp.max(peaks, axis=0), own_high)
    weights_src = jnp.exp(peaks - highest[None])
    own_factor = jnp.exp(own_high - highest)
    totals = jnp.sum(amounts * weights_src, axis=0) + own_total * own_factor
    weighted_sum = (
        jnp.sum(vectors * weights_src[..., None], axis=0) + own_sum * own_factor[..., None]
    )
    attention = finish(totals, weighted_sum, kv_heads, group_size, step_count)
    every_head = lax.all_gather(attention, "ctx", axis=0, tiled=True)
    flattened = every_head.reshape(request_count * step_count, -1)
    kept_rows = request_count * step_count // lax.axis_size("tp")
    result_rows = lax.psum_scatter(
        jnp.dot(flattened, out_weight, preferred_element_type=jnp.float32),
        "tp",
        scatter_dimension=0,
        tiled=True,
    )
    return result_rows.astype(jnp.bfloat16).reshape(kept_rows // step_count, step_count, -1)


def solution(mesh):
    return jax.shard_map(
        per_device,
        mesh=mesh,
        in_specs=(
            P("ctx", None, "tp", None),
            P("ctx", None, "tp", None),
            P("ctx", None, "tp", None),
            P("ctx", None, "tp", None),
            P("ctx", None, "tp", None),
            P("ctx"),
            P(),
            P("tp", "ctx"),
        ),
        out_specs=P("tp", None, "ctx"),
        check_vma=False,
    )
```

profile of v0, /device:TPU:0, one launch (start us, length us, event | category | flops | bytes accessed | tf_op | source)
XLA Modules:
  0.0 222.3 jit_solution(1465230819509264900)
XLA Ops:
  6.5 0.7 all-gather.3.cloned.1.call-update
  8.7 1.4 gather_fusion
  10.3 42.2 %all-gather.3.cloned.1.call-done = bf16[64,4,16,128]{3,2,1,0:T(8,128)(2,1)} async-done(((bf16[8,4,16,128]{3,2,1,0:T(8,128)(2,1)}), bf16[64,4,16,128]{3,2,1,0:T(8,128)(2,1)}) %all-gather.3.cloned.1.call-update) | async-done | bytes 1048592 | tf_op jit(solution)/shard_map/all_gather | solution.py:50
  52.5 2.0 gather_fusion.1
  54.5 8.2 %bitcast_reduce_fusion = (f32[64,2,8,4]{2,3,1,0:T(4,128)S(1)}, f32[64,2,4,8,256]{4,3,2,1,0:T(8,128)}) fusion(pred[64,256]{1,0:T(8,128)(4,1)S(1)} %fusion.15, bf16[64,256,2,128,1]{3,2,1,0,4:T(2,128)(2,1)} %bitcast.60, bf16[64,4,16,128]{3,2,1,0:T(8,128)(2,1)S(1)} %gather_fusion.1), kind=kOutput, calls=%fused_computation.8 | convolution fusion | flops 271577088 | bytes 13664256 | tf_op jit(solution)/shard_map/ptkgd,pbkd->pkgtb/dot_general | solution.py:11
  62.9 0.7 select_reduce_fusion
  64.2 3.3 %convert_reduce_fusion = f32[64,2,8,4]{2,3,1,0:T(4,128)S(1)} fusion(f32[64,2,8,4]{2,3,1,0:T(4,128)S(1)} %get-tuple-element.12, f32[64,2,4,8,256]{4,3,2,1,0:T(8,128)} %get-tuple-element.13, pred[64,256]{1,0:T(8,128)(4,1)S(1)} %fusion.15), kind=kLoop, calls=%fused_computation.12 | loop fusion | flops 7335936 | bytes 4243456 | tf_op jit(solution)/shard_map/reduce_sum | solution.py:19
  68.8 3.3 %all-to-all-start.2 = ((f32[8,1,512]{2,1,0:T(1,128)}), f32[8,1,512]{2,1,0:T(1,128)S(1)}, u32[]{:S(2)}, u32[]{:S(2)}) async-start(f32[8,1,512]{2,1,0:T(1,128)} %reshape.250), calls=%async_computation.2 | async-start | bytes 32768 | tf_op jit(solution)/shard_map/all_to_all | solution.py:90
  72.1 6.2 %fusion = f32[64,2,8,4,128]{4,2,3,1,0:T(8,128)S(1)} fusion(bf16[64,256,2,128,1]{3,2,1,0,4:T(2,128)(2,1)} %bitcast.75, f32[64,2,4,8,256]{4,3,2,1,0:T(8,128)} %get-tuple-element.13, f32[64,2,8,4]{2,3,1,0:T(4,128)S(1)} %get-tuple-element.12, pred[64,256]{1,0:T(8,128)(4,1)S(1)} %fusion.15), kind=kOutput, calls=%fused_computation.3 | convolution fusion | flops 273678336 | bytes 14712832 | tf_op jit(solution)/shard_map/pkgtb,pbkd->pkgtd/dot_general | solution.py:20
  78.3 1.2 copy.112
  80.8 5.9 %all-to-all-start.1 = ((f32[8,1,512]{2,1,0:T(1,128)}), f32[8,1,512]{2,1,0:T(1,128)S(1)}, u32[]{:S(2)}, u32[]{:S(2)}) async-start(f32[8,1,512]{2,1,0:T(1,128)} %reshape.248), calls=%async_computation.1 | async-start | bytes 32768 | tf_op jit(solution)/shard_map/all_to_all | solution.py:89
  86.8 1.2 fusion.21
  88.1 2.6 %copy.118 = f32[64,64,128]{2,1,0:T(8,128)} copy(f32[64,64,128]{2,0,1:T(8,128)S(1)} %fusion.21) | data formatting | bytes 4194304 | tf_op jit(solution)/shard_map/pr,pqd->rqd/dot_general | solution.py:85
  90.6 2.7 %all-to-all-done.1 = f32[8,1,512]{2,1,0:T(1,128)S(1)} async-done(((f32[8,1,512]{2,1,0:T(1,128)}), f32[8,1,512]{2,1,0:T(1,128)S(1)}, u32[]{:S(2)}, u32[]{:S(2)}) %all-to-all-start.1) | async-done | bytes 16416 | tf_op jit(solution)/shard_map/all_to_all | solution.py:89
  93.4 3.6 %all-to-all-start = ((f32[64,64,128]{2,1,0:T(8,128)}), f32[64,64,128]{2,1,0:T(8,128)S(1)}, u32[]{:S(2)}, u32[]{:S(2)}) async-start(f32[64,64,128]{2,1,0:T(8,128)} %copy.118), calls=%async_computation | async-start | bytes 4194304 | tf_op jit(solution)/shard_map/all_to_all | solution.py:91
  100.8 41.8 %all-to-all-done = f32[64,64,128]{2,1,0:T(8,128)S(1)} async-done(((f32[64,64,128]{2,1,0:T(8,128)}), f32[64,64,128]{2,1,0:T(8,128)S(1)}, u32[]{:S(2)}, u32[]{:S(2)}) %all-to-all-start) | async-done | bytes 2097184 | tf_op jit(solution)/shard_map/all_to_all | solution.py:91
  142.5 0.7 multiply_reduce_fusion
  143.7 0.7 convert_element_type.31
  144.5 39.2 %all-gather.5.cloned.1.call-done = bf16[64,4,2048]{2,0,1:T(8,128)(2,1)} async-done(((bf16[8,4,2048]{2,0,1:T(8,128)(2,1)}), bf16[64,4,2048]{2,0,1:T(8,128)(2,1)}) %all-gather.5.cloned.1.call-update) | async-done | bytes 1048592 | tf_op jit(solution)/shard_map/all_gather | solution.py:106
  183.6 2.0 copy.133
  185.9 4.4 %fusion.37 = f32[256,1024]{1,0:T(8,128)} fusion(bf16[256,2048]{1,0:T(8,128)(2,1)S(1)} %reshape.213, bf16[2048,1024]{1,0:T(8,128)(2,1)} %param.15), kind=kOutput, calls=%fused_computation.64 | convolution fusion | flops 1073741824 | bytes 6291456 | tf_op jit(solution)/shard_map/dot_general | solution.py:110
  190.4 23.7 %reduce-scatter.2.cloned.1.call-done = f32[64,1024]{1,0:T(8,128)} async-done(((f32[256,1024]{1,0:T(8,128)}), f32[64,1024]{1,0:T(8,128)}) %reduce-scatter.2.cloned.1.call-update) | async-done | bytes 262160 | tf_op jit(solution)/shard_map/reduce_scatter | solution.py:109
  214.1 1.0 convert_element_type.32
  215.1 0.7 reshape.214
  (51 shorter events, 9.4 us)
Async XLA Ops:
  6.5 136.7 %copy-start = (bf16[8,4,2,128]{3,2,1,0:T(2,128)(2,1)S(1)}, bf16[8,4,2,128]{3,2,1,0:T(2,128)(2,1)}, u32[]{:S(2)}) copy-start(bf16[8,4,2,128]{3,2,1,0:T(2,128)(2,1)} %param.10) | copy-start | bytes 49156
  6.5 46.0 %all-gather.3.cloned.1.call-start = ((), (), s32[]{:S(2)}) async-start(), calls=%async_computation.4 | async-start | bytes 1179648 | tf_op jit(solution)/shard_map/all_gather | solution.py:50
  68.8 12.0 %all-to-all-start.2 = ((f32[8,1,512]{2,1,0:T(1,128)}), f32[8,1,512]{2,1,0:T(1,128)S(1)}, u32[]{:S(2)}, u32[]{:S(2)}) async-start(f32[8,1,512]{2,1,0:T(1,128)} %reshape.250), calls=%async_computation.2 | async-start | bytes 32768 | tf_op jit(solution)/shard_map/all_to_all | solution.py:90
  80.8 12.5 %all-to-all-start.1 = ((f32[8,1,512]{2,1,0:T(1,128)}), f32[8,1,512]{2,1,0:T(1,128)S(1)}, u32[]{:S(2)}, u32[]{:S(2)}) async-start(f32[8,1,512]{2,1,0:T(1,128)} %reshape.248), calls=%async_computation.1 | async-start | bytes 32768 | tf_op jit(solution)/shard_map/all_to_all | solution.py:89
  88.0 9.2 %copy-start.1 = (bf16[8,4,16,128]{3,2,1,0:T(8,128)(2,1)S(1)}, bf16[8,4,16,128]{3,2,1,0:T(8,128)(2,1)}, u32[]{:S(2)}) copy-start(bf16[8,4,16,128]{3,2,1,0:T(8,128)(2,1)} %param.8) | copy-start | bytes 393220
  88.1 9.2 %copy-start.2 = (bf16[8,4,2,128]{3,2,1,0:T(2,128)(2,1)S(1)}, bf16[8,4,2,128]{3,2,1,0:T(2,128)(2,1)}, u32[]{:S(2)}) copy-start(bf16[8,4,2,128]{3,2,1,0:T(2,128)(2,1)} %param.9) | copy-start | bytes 49156
  93.4 49.2 %all-to-all-start = ((f32[64,64,128]{2,1,0:T(8,128)}), f32[64,64,128]{2,1,0:T(8,128)S(1)}, u32[]{:S(2)}, u32[]{:S(2)}) async-start(f32[64,64,128]{2,1,0:T(8,128)} %copy.118), calls=%async_computation | async-start | bytes 4194304 | tf_op jit(solution)/shard_map/all_to_all | solution.py:91
  97.0 86.6 %all-gather.5.cloned.1.call-start = ((), (), s32[]{:S(2)}) async-start(), calls=%async_computation.5 | async-start | bytes 1179648 | tf_op jit(solution)/shard_map/all_gather | solution.py:106
  144.4 69.7 %reduce-scatter.2.cloned.1.call-start = ((), (), s32[]{:S(2)}) async-start(), calls=%async_computation.6 | async-start | bytes 1310720 | tf_op jit(solution)/shard_map/reduce_scatter | solution.py:109
Sparse Core Ops, SparseCore 0:
  9.5 42.9 all-gather.2
  144.5 39.0 all-gather.4
  190.5 23.5 reduce-scatter.1
where the time goes:
time: 223 us; the launch traced here: 222 us
  waiting for transfers between devices  150 us (67%)
  matrix products  21.3 us (10%)
  local copies, waits for them, and re-layouts  14.7 us (7%)
  between operations  13.3 us (6%)
  starting transfers between devices  13.1 us (6%)
  other arithmetic  9.44 us (4%)
    all_gather x1, waiting for transfers between devices, per_device(): every_query = lax.all_gather(queries, 'ctx', axis=0, tiled=True)  42.2 us
    all_to_all x1, waiting for transfers between devices, per_device(): lax.all_to_all(req_sum, 'ctx', split_axis=0, concat_axis=0, tiled=True)  41.8 us
    all_gather x1, waiting for transfers between devices, per_device(): every_head = lax.all_gather(attention, 'ctx', axis=0, tiled=True)  39.2 us
    reduce_scatter x1, waiting for transfers between devices, per_device(): lax.psum_scatter(jnp.dot(flattened, out_weight, preferred_element_type=jn...  23.7 us
    dot_general x2, matrix products, block_partial(): jnp.einsum(pattern[0], decode_query_rows, gathered_keys, preferred_elemen...  8.9 us
    dot_general x2, matrix products, block_partial(): jnp.einsum(pattern[1], softmax_weights, gathered_values, preferred_elemen...  6.54 us
    all_to_all x1, starting transfers between devices, per_device(): lax.all_to_all(req_high, 'ctx', split_axis=0, concat_axis=0, tiled=True)  5.94 us
  transfers between devices with their start and end apart: 6, of which 5 were waited for; matrix products, arithmetic and copies ran while one was open for 9% of the time, Pallas kernels for 0%

commit v1 on v0

v1 whole, which is shorter than its diff:
```python
import functools
import math

import jax
import jax.numpy as jnp
from jax import lax
from jax.experimental import pallas as pl
from jax.experimental.pallas import tpu as pltpu
from jax.sharding import PartitionSpec as P

MAXB = 128
GROUP = 4
NEG = -1e30
LOG2E = math.log2(math.e)
F32 = jnp.float32
BF16 = jnp.bfloat16

NT = (((1,), (1,)), ((), ()))


def request_kernel(owned, rows, block_len, round_ref, slot_ref, len_ref, q_ref, out_ref, count):
    me = lax.axis_index("ctx")
    for r in range(owned):
        count[r] = 0

    def tally(s, carry):
        code = slot_ref[s]
        local = lax.div(code, MAXB) - me * owned

        @pl.when((code >= 0) & (local >= 0) & (local < owned))
        def _():
            count[local] = count[local] + 1

        return carry

    lax.fori_loop(0, slot_ref.shape[0], tally, 0)
    seen = jnp.int32(0)
    pick = jnp.int32(-1)
    for r in range(owned):
        blocks = lax.div(len_ref[me * owned + r] + (block_len - 1), block_len)
        lent = count[r] < blocks
        pick = jnp.where(lent & (seen == round_ref[0]), r, pick)
        seen = seen + lent.astype(jnp.int32)
    row = lax.broadcasted_iota(jnp.int32, (16, 128), 0)
    info = jnp.where(row == 0, seen, pick).astype(F32).astype(BF16)
    body = q_ref[jnp.maximum(pick, 0)]
    for c in range(out_ref.shape[0]):
        out_ref[c, pl.ds(0, rows), :] = body
        out_ref[c, pl.ds(rows, 16), :] = info


def attend(
    foreign, owned, kv, group, slot_ref, len_ref, query_of,
    k_hbm, v_hbm, kbuf, vbuf, ksem, vsem, order, m_acc, l_acc, a_acc,
):
    me = lax.axis_index("ctx")
    width, head = kbuf.shape[1:]
    block_len = width // kv
    rows = m_acc.shape[1]
    heads = group * kv
    coef = head ** -0.5 * LOG2E

    def begin(s, n):
        code = slot_ref[s]
        is_own = lax.div(lax.div(code, MAXB), owned) == me
        mine = (code >= 0) & (jnp.logical_not(is_own) if foreign else is_own)

        @pl.when(mine)
        def _():
            order[n] = s
            pltpu.make_async_copy(k_hbm.at[s], kbuf.at[n], ksem.at[n]).start()
            pltpu.make_async_copy(v_hbm.at[s], vbuf.at[n], vsem.at[n]).start()

        return n + mine.astype(jnp.int32)

    n = lax.fori_loop(0, slot_ref.shape[0], begin, jnp.int32(0))
    col = lax.broadcasted_iota(jnp.int32, (rows, width), 1)
    row = lax.broadcasted_iota(jnp.int32, (rows, width), 0)
    same = (col % kv) == (row % heads) // group
    place = jnp.where(same, col, width * 2)

    def step(it, carry):
        for g in range(GROUP):
            i = it * GROUP + g

            @pl.when(i < n)
            def _():
                pltpu.make_async_copy(k_hbm.at[0], kbuf.at[i], ksem.at[i]).wait()
                pltpu.make_async_copy(v_hbm.at[0], vbuf.at[i], vsem.at[i]).wait()

        parts = []
        for g in range(GROUP):
            i = it * GROUP + g
            slot = jnp.minimum(i, n - 1)
            code = slot_ref[order[slot]]
            r = lax.div(code, MAXB)
            valid = jnp.clip(len_ref[r] - (code - r * MAXB) * block_len, 0, block_len)
            valid = jnp.where(i < n, valid, 0) * kv
            e = jnp.int32(0) if foreign else r - me * owned
            scores = lax.dot_general(query_of(e), kbuf[slot], NT, preferred_element_type=F32)
            scores = jnp.where(place < valid, scores, NEG)
            high = jnp.max(scores, axis=1, keepdims=True)
            weights = jnp.exp2((scores - high) * coef).astype(BF16)
            rounded = weights.astype(F32)
            total = rounded[:, :128]
            for c in range(1, width // 128):
                total = total + rounded[:, c * 128 : (c + 1) * 128]
            summed = jnp.dot(weights, vbuf[slot], preferred_element_type=F32)
            parts.append((e, high, total, summed))
        for e, high, total, summed in parts:
            before = m_acc[e]
            peak = jnp.maximum(before, high)
            keep = jnp.exp2((before - peak) * coef)
            add = jnp.exp2((high - peak) * coef)
            m_acc[e] = peak
            l_acc[e] = l_acc[e] * keep + total * add
            a_acc[e] = a_acc[e] * keep + summed * add
        return carry

    lax.fori_loop(0, lax.div(n + GROUP - 1, GROUP), step, 0)
    return n


def own_kernel(
    owned, steps, kv, group, slot_ref, len_ref, q_ref, nk_ref, nv_ref, k_hbm, v_hbm,
    out_ref, lse_ref, kbuf, vbuf, ksem, vsem, order, m_acc, l_acc, a_acc,
):
    rows, head = q_ref.shape[1:]
    heads = kv * group
    coef = head ** -0.5 * LOG2E
    fresh = nk_ref.shape[0]
    col = lax.broadcasted_iota(jnp.int32, (rows, fresh), 1)
    row = lax.broadcasted_iota(jnp.int32, (rows, fresh), 0)
    seen = ((col % kv) == (row % heads) // group) & (lax.div(col, kv) % steps <= lax.div(row, heads))
    lane = lax.broadcasted_iota(jnp.int32, (rows, 128), 1)
    nk = nk_ref[...]
    nv = nv_ref[...]
    for r in range(owned):
        scores = lax.dot_general(q_ref[r], nk, NT, preferred_element_type=F32)
        ok = seen & (lax.div(col, kv * steps) == r)
        scores = jnp.where(ok, scores, NEG)
        high = jnp.max(scores, axis=1, keepdims=True)
        weights = jnp.where(ok, jnp.exp2((scores - high) * coef), 0.0).astype(BF16)
        total = jnp.sum(weights.astype(F32), axis=1, keepdims=True)
        m_acc[r] = jnp.broadcast_to(high, (rows, 128))
        l_acc[r] = jnp.where(lane == 0, total, 0.0)
        a_acc[r] = jnp.dot(weights, nv, preferred_element_type=F32)
    attend(
        False, owned, kv, group, slot_ref, len_ref, lambda e: q_ref[e],
        k_hbm, v_hbm, kbuf, vbuf, ksem, vsem, order, m_acc, l_acc, a_acc,
    )
    table = jnp.zeros((rows, 128), F32)
    for r in range(owned):
        total = jnp.sum(l_acc[r], axis=1, keepdims=True)
        out_ref[r] = (a_acc[r] / total).astype(BF16)
        table = jnp.where(lane % 32 == r, m_acc[r] * coef + jnp.log(total) * LOG2E, table)
    lse_ref[...] = table


def lent_kernel(
    owned, kv, group, slot_ref, len_ref, got_ref, lse_ref, k_hbm, v_hbm,
    out_ref, kbuf, vbuf, ksem, vsem, order, m_acc, l_acc, a_acc,
):
    rows, head = out_ref.shape[1:]
    coef = head ** -0.5 * LOG2E
    me = lax.axis_index("ctx")

    def find(s, rid):
        code = slot_ref[s]
        r = lax.div(code, MAXB)
        return jnp.where((code >= 0) & (lax.div(r, owned) != me), r, rid)

    rid = lax.fori_loop(0, slot_ref.shape[0], find, jnp.int32(0))
    owner = lax.div(rid, owned)
    m_acc[0] = jnp.full((rows, 128), NEG, F32)
    l_acc[0] = jnp.zeros((rows, 128), F32)
    a_acc[0] = jnp.zeros((rows, head), F32)
    attend(
        True, owned, kv, group, slot_ref, len_ref, lambda e: got_ref[owner, pl.ds(0, rows), :],
        k_hbm, v_hbm, kbuf, vbuf, ksem, vsem, order, m_acc, l_acc, a_acc,
    )
    total = jnp.sum(l_acc[0], axis=1, keepdims=True)
    some = total > 0.0
    total = jnp.where(some, total, 1.0)
    out_ref[0] = (a_acc[0] / total).astype(BF16)
    lse = jnp.where(some, m_acc[0] * coef + jnp.log(total) * LOG2E, NEG)
    lane = lax.broadcasted_iota(jnp.int32, (rows, 128), 1)
    table = jnp.where(lane % 32 == owned, lse, lse_ref[...])
    table = jnp.where(lane % 32 == owned + 1, rid.astype(F32), table)
    second = table - table.astype(BF16).astype(F32)
    third = second - second.astype(BF16).astype(F32)
    out_ref[1] = jnp.where(lane < 32, table, jnp.where(lane < 64, second, third)).astype(BF16)


def project_kernel(
    owned, steps, heads, sources, parts, lent_ref, *refs
):
    pieces = refs[:sources]
    w_hbm, send_ref, keep_ref, full, lse, flat, wbuf, wsem = refs[sources:]
    me = lax.axis_index("ctx")
    mine = lax.axis_index("tp")
    rows = steps * heads
    head = full.shape[1]
    span = owned * rows
    per = sources // parts
    copy = pltpu.make_async_copy(w_hbm, wbuf, wsem)
    copy.start()

    def spot(c):
        return (lax.div(c, per) ^ mine) * per + lax.rem(c, per)

    lane = lax.broadcasted_iota(jnp.int32, (rows, 128), 1)
    for d in range(sources):
        start = pl.multiple_of(spot(me ^ d) * span, span)
        full[pl.ds(start, span), :] = pieces[d][...].astype(F32).reshape(span, head)
    rids = []
    for d in range(sources):
        packed = lent_ref[d, 1].astype(F32)
        table = packed + pltpu.roll(packed, 96, 1) + pltpu.roll(packed, 64, 1)
        lse[d] = table
        rids.append(jnp.max(jnp.where(lane[:8] == owned + 1, table[:8], -1.0)).astype(jnp.int32))
    for d in range(sources):
        c = lax.div(rids[d], owned)
        r = lax.rem(rids[d], owned)
        start = pl.multiple_of((spot(c) * owned + r) * rows, rows)
        theirs = lse[c]
        left = jnp.sum(jnp.where(lane == r, theirs, 0.0), axis=1, keepdims=True)
        right = jnp.sum(jnp.where(lane == owned, lse[d], 0.0), axis=1, keepdims=True)
        peak = jnp.maximum(left, right)
        w_left = jnp.exp2(left - peak)
        w_right = jnp.exp2(right - peak)
        total = w_left + w_right
        full[pl.ds(start, rows), :] = full[pl.ds(start, rows), :] * (w_left / total) + lent_ref[
            d, 0
        ].astype(F32) * (w_right / total)
        lse[c] = jnp.where(lane == r, peak + jnp.log(total) * LOG2E, theirs)
    count = sources * owned * steps
    for h in range(heads):
        flat[:, h * head : (h + 1) * head] = full[pl.ds(h, count, stride=heads), :].astype(BF16)
    copy.wait()
    result = jnp.dot(flat[...], wbuf[...], preferred_element_type=F32).astype(BF16)
    kept = count // parts
    for b in range(parts):
        target = keep_ref if b % 2 == 0 else send_ref
        target[b // 2] = result[b * kept : (b + 1) * kept]


def smem():
    return pl.BlockSpec(memory_space=pltpu.SMEM)


def vmem():
    return pl.BlockSpec(memory_space=pltpu.VMEM)


def hbm():
    return pl.BlockSpec(memory_space=pltpu.HBM)


def per_device(
    queries, new_keys, new_values, key_pool, value_pool, slot_block, lengths, out_weight
):
    owned, steps, heads, head = queries.shape
    kv = new_keys.shape[2]
    group = heads // kv
    slots, block_len = key_pool.shape[:2]
    sources = lax.axis_size("ctx")
    parts = lax.axis_size("tp")
    rows = steps * heads
    cols = out_weight.shape[1]
    q = queries.reshape(owned, rows, head)
    nk = new_keys.reshape(owned * steps * kv, head)
    nv = new_values.reshape(owned * steps * kv, head)
    keys = key_pool.reshape(slots, block_len * kv, head)
    values = value_pool.reshape(slots, block_len * kv, head)

    def ask(turn):
        message = pl.pallas_call(
            functools.partial(request_kernel, owned, rows, block_len),
            out_shape=jax.ShapeDtypeStruct((sources, rows + 16, head), BF16),
            in_specs=[smem(), smem(), smem(), vmem()],
            out_specs=vmem(),
            scratch_shapes=[pltpu.SMEM((owned,), jnp.int32)],
            name="ask",
        )(turn, slot_block, lengths, q)
        return lax.all_to_all(message, "ctx", split_axis=0, concat_axis=0, tiled=True)

    def buffers(sets):
        return [
            pltpu.VMEM((slots, block_len * kv, head), BF16),
            pltpu.VMEM((slots, block_len * kv, head), BF16),
            pltpu.SemaphoreType.DMA((slots,)),
            pltpu.SemaphoreType.DMA((slots,)),
            pltpu.SMEM((slots,), jnp.int32),
            pltpu.VMEM((sets, rows, 128), F32),
            pltpu.VMEM((sets, rows, 128), F32),
            pltpu.VMEM((sets, rows, head), F32),
        ]

    got = ask(jnp.zeros((1,), jnp.int32))
    own, lse = pl.pallas_call(
        functools.partial(own_kernel, owned, steps, kv, group),
        out_shape=(
            jax.ShapeDtypeStruct((owned, rows, head), BF16),
            jax.ShapeDtypeStruct((rows, 128), F32),
        ),
        in_specs=[smem(), smem(), vmem(), vmem(), vmem(), hbm(), hbm()],
        out_specs=(vmem(), vmem()),
        scratch_shapes=buffers(owned),
        name="own",
        compiler_params=pltpu.CompilerParams(vmem_limit_bytes=40 * 2**20),
    )(slot_block, lengths, q, nk, nv, keys, values)

    rounds = jnp.max(got[:, rows, 0]).astype(jnp.int32)
    here = lax.axis_index("ctx")
    request = slot_block // MAXB
    lent = (slot_block >= 0) & (request // owned != here)
    wanted = jnp.max(jnp.where(lent, request % owned, -1)).astype(F32)

    def more(state):
        return state[0] < rounds

    def next_round(state):
        turn, held = state
        fresh = ask(turn.reshape(1))
        match = fresh[:, rows + 1, 0].astype(F32) == wanted
        return turn + 1, jnp.where(match[:, None, None], fresh, held)

    _, got = lax.while_loop(more, next_round, (jnp.int32(1), got))

    partial = pl.pallas_call(
        functools.partial(lent_kernel, owned, kv, group),
        out_shape=jax.ShapeDtypeStruct((2, rows, head), BF16),
        in_specs=[smem(), smem(), vmem(), vmem(), hbm(), hbm()],
        out_specs=vmem(),
        scratch_shapes=buffers(1),
        name="lent",
        compiler_params=pltpu.CompilerParams(vmem_limit_bytes=40 * 2**20),
    )(slot_block, lengths, got, lse, keys, values)

    pieces = [own]
    for d in range(1, sources):
        bit = 1 if d % 2 else d
        pieces.append(
            lax.ppermute(pieces[d ^ bit], "ctx", [(i, i ^ bit) for i in range(sources)])
        )
    spread = lax.all_to_all(
        jnp.broadcast_to(partial[None], (sources,) + partial.shape),
        "ctx", split_axis=0, concat_axis=0, tiled=True,
    )
    count = sources * owned * steps
    kept = count // parts
    send, keep = pl.pallas_call(
        functools.partial(project_kernel, owned, steps, heads, sources, parts),
        out_shape=(
            jax.ShapeDtypeStruct((parts // 2, kept, cols), BF16),
            jax.ShapeDtypeStruct((parts // 2, kept, cols), BF16),
        ),
        in_specs=[vmem()] * (1 + sources) + [hbm()],
        out_specs=(vmem(), vmem()),
        scratch_shapes=[
            pltpu.VMEM((sources * owned * rows, head), F32),
            pltpu.VMEM((sources, rows, 128), F32),
            pltpu.VMEM((count, heads * head), BF16),
            pltpu.VMEM(out_weight.shape, BF16),
            pltpu.SemaphoreType.DMA,
        ],
        name="project",
        compiler_params=pltpu.CompilerParams(vmem_limit_bytes=48 * 2**20),
    )(spread, *pieces, out_weight)

    bit = 1
    while True:
        other = lax.ppermute(send, "tp", [(i, i ^ bit) for i in range(parts)])
        held = keep.astype(F32) + other.astype(F32)
        bit *= 2
        if bit == parts:
            break
        held = held.reshape((held.shape[0] // 2, 2) + held.shape[1:])
        send, keep = held[:, 1].astype(BF16), held[:, 0]
    return held.astype(BF16).reshape(kept // steps, steps, cols)


def solution(mesh):
    return jax.shard_map(
        per_device,
        mesh=mesh,
        in_specs=(
            P("ctx", None, "tp", None),
            P("ctx", None, "tp", None),
            P("ctx", None, "tp", None),
            P("ctx", None, "tp", None),
            P("ctx", None, "tp", None),
            P("ctx"),
            P(),
            P("tp", "ctx"),
        ),
        out_specs=P("tp", None, "ctx"),
        check_vma=False,
    )
```

time: 223 us -> 108 us (0.48)
  waiting for transfers between devices: 150 us -> 22 us
  Pallas kernels: 0 us -> 45 us
  matrix products: 21.3 us -> 0 us
  between operations: 13.3 us -> 1.38 us
  starting transfers between devices: 13.1 us -> 24 us
  other arithmetic: 9.44 us -> 2.05 us
  local copies, waits for them, and re-layouts: 14.7 us -> 11.9 us
    all_gather x2 -> x0, waiting for transfers between devices: 81.4 us -> none  [the longest x1 42.2 us: per_device(): every_query = lax.all_gather(queries, 'ctx', axis=0, tiled=True)]
    pallas_call x0 -> x4, Pallas kernels: none -> 45 us  [the longest x1 34.7 us: per_device(): pl.pallas_call(functools.partial(own_kernel, owned, steps, kv, group), ou...]
    all_to_all x3 -> x2, waiting for transfers between devices: 44.5 us -> 0.01 us  [the longest x1 0.01 us: ask(): lax.all_to_all(message, 'ctx', split_axis=0, concat_axis=0, tiled=True)]
    reduce_scatter x1 -> x0, waiting for transfers between devices: 23.7 us -> none  [per_device(): lax.psum_scatter(jnp.dot(flattened, out_weight, preferred_element_type=jn...]
    ppermute x0 -> x9, waiting for transfers between devices: none -> 22 us  [the longest x7 16.5 us: per_device(): lax.ppermute(pieces[d ^ bit], 'ctx', [(i, i ^ bit) for i in range(sources)])]
    dot_general x7 -> x0, matrix products: 21.3 us -> none  [the longest x2 8.9 us: block_partial(): jnp.einsum(pattern[0], decode_query_rows, gathered_keys, preferred_elemen...]
    ppermute x0 -> x9, starting transfers between devices: none -> 11.6 us  [the longest x7 9.9 us: per_device(): lax.ppermute(pieces[d ^ bit], 'ctx', [(i, i ^ bit) for i in range(sources)])]
    unnamed x10 -> x16, local copies, waits for them, and re-layouts: 1.55 us -> 10.4 us
  transfers between devices with their start and end apart: 6 -> 11, of which waited for: 5 -> 6; matrix products, arithmetic and copies ran while one was open for 9% -> 1% of each run, Pallas kernels for 0% -> 33%
where the time goes in v1:
time: 108 us; the launch traced here: 106 us
  Pallas kernels  45 us (42%)
  starting transfers between devices  24 us (22%)
  waiting for transfers between devices  22 us (20%)
  local copies, waits for them, and re-layouts  11.9 us (11%)
  other arithmetic  2.05 us (2%)
  between operations  1.38 us (1%)
    pallas_call x1, Pallas kernels, per_device(): pl.pallas_call(functools.partial(own_kernel, owned, steps, kv, group), ou...  34.7 us
    ppermute x7, waiting for transfers between devices, per_device(): lax.ppermute(pieces[d ^ bit], 'ctx', [(i, i ^ bit) for i in range(sources)])  16.5 us
    unnamed x16, local copies, waits for them, and re-layouts  10.4 us
    ppermute x7, starting transfers between devices, per_device(): lax.ppermute(pieces[d ^ bit], 'ctx', [(i, i ^ bit) for i in range(sources)])  9.9 us
    all_to_all x1, starting transfers between devices, ask(): lax.all_to_all(message, 'ctx', split_axis=0, concat_axis=0, tiled=True)  7.28 us
    ppermute x2, waiting for transfers between devices, per_device(): other = lax.ppermute(send, 'tp', [(i, i ^ bit) for i in range(parts)])  5.52 us
    all_to_all x1, starting transfers between devices, per_device(): lax.all_to_all(jnp.broadcast_to(partial[None], (sources,) + partial.shape...  5.1 us
    pallas_call x1, Pallas kernels, per_device(): pl.pallas_call(functools.partial(lent_kernel, owned, kv, group), out_shap...  3.91 us
  transfers between devices with their start and end apart: 11, of which 6 were waited for; matrix products, arithmetic and copies ran while one was open for 1% of the time, Pallas kernels for 33%

profile of v1, /device:TPU:0, one launch (start us, length us, event | category | flops | bytes accessed | tf_op | source)
XLA Modules:
  0.0 106.3 jit_solution(12438326365049991790)
XLA Ops:
  0.0 2.7 %ask.2 = bf16[8,80,128]{2,1,0:T(8,128)(2,1)} custom-call(s32[1]{0:T(128)} %constant.44.clone.1.round_ref, s32[64]{0:T(128)} %slot_ref.5, s32[64]{0:T(128)} %len_ref.5, bf16[8,64,128]{2,1,0:T(8,128)(2,1)} %bitcast.24), custom_call_target="tpu_custom_call" | custom-call | tf_op jit(solution)/shard_map/ask/pallas_call | solution.py:278
  2.7 7.3 %all-to-all-start.1 = ((bf16[8,80,128]{2,1,0:T(8,128)(2,1)}), bf16[8,80,128]{2,1,0:T(8,128)(2,1)S(1)}, u32[]{:S(2)}, u32[]{:S(2)}) async-start(bf16[8,80,128]{2,1,0:T(8,128)(2,1)} %ask.2), calls=%async_computation.1 | async-start | bytes 327680 | tf_op jit(solution)/shard_map/all_to_all | solution.py:286
  10.0 1.4 %fusion.3 = s32[]{:T(128)} fusion(s32[64]{0:T(128)} %slot_ref.5, s32[]{:T(128)S(6)} %axis_index.15), kind=kLoop, calls=%fused_computation.20 | loop fusion | flops 2495 | bytes 264 | tf_op jit(solution)/shard_map/reduce_max | solution.py:318
  12.1 3.4 %copy-done = bf16[64,256,2,128]{3,2,1,0:T(2,128)(2,1)S(1)} copy-done((bf16[64,256,2,128]{3,2,1,0:T(2,128)(2,1)S(1)}, bf16[64,256,2,128]{3,2,1,0:T(2,128)(2,1)}, u32[]{:S(2)}) %copy-start) | copy-done | bytes 8388632
  15.5 0.7 copy-done.3
  16.2 0.7 copy-done.4
  16.9 34.7 %own.1 = (bf16[8,64,128]{2,1,0:T(8,128)(2,1)S(1)}, f32[64,128]{1,0:T(8,128)S(1)}) custom-call(s32[64]{0:T(128)} %slot_ref.5, s32[64]{0:T(128)} %len_ref.5, bf16[8,64,128]{2,1,0:T(8,128)(2,1)} %bitcast.25, bf16[64,128]{1,0:T(8,128)(2,1)S(1)} %bitcast.20, bf16[64,128]{1,0:T(8,128)(2,1)S(1)} %bitcast.21, bf16[64,512,128]{2,1,0:T(8,128)(2,1)S(1)} %bitcast.18, ...), custom_call_target="tpu_custom_call" | custom-call | tf_op jit(solution)/shard_map/own/pallas_call | solution.py:301
  52.8 3.4 %copy-done.1 = bf16[64,256,2,128]{3,2,1,0:T(2,128)(2,1)S(1)} copy-done((bf16[64,256,2,128]{3,2,1,0:T(2,128)(2,1)S(1)}, bf16[64,256,2,128]{3,2,1,0:T(2,128)(2,1)}, u32[]{:S(2)}) %copy-start.1) | copy-done | bytes 8388632
  56.2 3.9 %lent.1 = bf16[2,64,128]{2,1,0:T(8,128)(2,1)S(1)} custom-call(s32[64]{0:T(128)S(1)} %get-tuple-element.159, s32[64]{0:T(128)S(1)} %get-tuple-element.160, bf16[8,80,128]{2,1,0:T(8,128)(2,1)S(1)} %get-tuple-element.47.got_ref, f32[64,128]{1,0:T(8,128)S(1)} %get-tuple-element.48.lse_ref, bf16[64,512,128]{2,1,0:T(8,128)(2,1)S(1)} %bitcast.19, ...), custom_call_target="tpu_custom_call" | custom-call | tf_op jit(solution)/shard_map/lent/pallas_call | solution.py:331
  60.1 0.7 broadcast_in_dim.19
  60.8 5.1 %all-to-all-start.2 = ((bf16[8,2,64,128]{3,2,1,0:T(8,128)(2,1)}), bf16[8,2,64,128]{3,2,1,0:T(8,128)(2,1)S(1)}, u32[]{:S(2)}, u32[]{:S(2)}) async-start(bf16[8,2,64,128]{3,2,1,0:T(8,128)(2,1)} %broadcast_in_dim.19), calls=%async_computation.2 | async-start | bytes 524288 | tf_op jit(solution)/shard_map/all_to_all | solution.py:347
  65.9 3.8 %collective-permute-start.5 = (bf16[8,64,128]{2,1,0:T(8,128)(2,1)S(1)}, bf16[8,64,128]{2,1,0:T(8,128)(2,1)S(1)}, u32[]{:S(2)}, u32[]{:S(2)}) collective-permute-start(bf16[8,64,128]{2,1,0:T(8,128)(2,1)S(1)} %get-tuple-element.49.refs_0_), channel_id=1, source_target_pairs={{0,24},{4,28},{8,16},{12,20},{16,8},{20,12},{24,0},{28,4},{1,25},{... | collective-permute-start | bytes 393224 | tf_op jit(solution)/shard_map/ppermute | solution.py:345
  70.3 2.0 %collective-permute-start = (bf16[8,64,128]{2,1,0:T(8,128)(2,1)S(1)}, bf16[8,64,128]{2,1,0:T(8,128)(2,1)S(1)}, u32[]{:S(2)}, u32[]{:S(2)}) collective-permute-start(bf16[8,64,128]{2,1,0:T(8,128)(2,1)S(1)} %get-tuple-element.49.refs_0_), channel_id=1, source_target_pairs={{0,4},{4,0},{8,12},{12,8},{16,20},{20,16},{24,28},{28,24},{1,5},{5... | collective-permute-start | bytes 393224 | tf_op jit(solution)/shard_map/ppermute | solution.py:345
  72.3 6.2 %collective-permute-done.5.refs_6_ = bf16[8,64,128]{2,1,0:T(8,128)(2,1)S(1)} collective-permute-done((bf16[8,64,128]{2,1,0:T(8,128)(2,1)S(1)}, bf16[8,64,128]{2,1,0:T(8,128)(2,1)S(1)}, u32[]{:S(2)}, u32[]{:S(2)}) %collective-permute-start.5) | collective-permute-done | bytes 131104 | tf_op jit(solution)/shard_map/ppermute | solution.py:345
  78.5 1.5 %collective-permute-start.6 = (bf16[8,64,128]{2,1,0:T(8,128)(2,1)S(1)}, bf16[8,64,128]{2,1,0:T(8,128)(2,1)S(1)}, u32[]{:S(2)}, u32[]{:S(2)}) collective-permute-start(bf16[8,64,128]{2,1,0:T(8,128)(2,1)S(1)} %collective-permute-done.5.refs_6_), channel_id=1, source_target_pairs={{0,4},{4,0},{8,12},{12,8},{16,20},{20,16},{24,28},{28,24},{1,5},{5... | collective-permute-start | bytes 393224 | tf_op jit(solution)/shard_map/ppermute | solution.py:345
  80.0 5.5 %collective-permute-done.3.refs_4_ = bf16[8,64,128]{2,1,0:T(8,128)(2,1)S(1)} collective-permute-done((bf16[8,64,128]{2,1,0:T(8,128)(2,1)S(1)}, bf16[8,64,128]{2,1,0:T(8,128)(2,1)S(1)}, u32[]{:S(2)}, u32[]{:S(2)}) %collective-permute-start.3) | collective-permute-done | bytes 131104 | tf_op jit(solution)/shard_map/ppermute | solution.py:345
  85.5 1.5 %collective-permute-start.4 = (bf16[8,64,128]{2,1,0:T(8,128)(2,1)S(1)}, bf16[8,64,128]{2,1,0:T(8,128)(2,1)S(1)}, u32[]{:S(2)}, u32[]{:S(2)}) collective-permute-start(bf16[8,64,128]{2,1,0:T(8,128)(2,1)S(1)} %collective-permute-done.3.refs_4_), channel_id=1, source_target_pairs={{0,4},{4,0},{8,12},{12,8},{16,20},{20,16},{24,28},{28,24},{1,5},{5... | collective-permute-start | bytes 393224 | tf_op jit(solution)/shard_map/ppermute | solution.py:345
  87.5 3.4 %collective-permute-done.4.refs_5_ = bf16[8,64,128]{2,1,0:T(8,128)(2,1)S(1)} collective-permute-done((bf16[8,64,128]{2,1,0:T(8,128)(2,1)S(1)}, bf16[8,64,128]{2,1,0:T(8,128)(2,1)S(1)}, u32[]{:S(2)}, u32[]{:S(2)}) %collective-permute-start.4) | collective-permute-done | bytes 131104 | tf_op jit(solution)/shard_map/ppermute | solution.py:345
  90.9 1.4 %collective-permute-done.2.refs_3_ = bf16[8,64,128]{2,1,0:T(8,128)(2,1)S(1)} collective-permute-done((bf16[8,64,128]{2,1,0:T(8,128)(2,1)S(1)}, bf16[8,64,128]{2,1,0:T(8,128)(2,1)S(1)}, u32[]{:S(2)}, u32[]{:S(2)}) %collective-permute-start.2) | collective-permute-done | bytes 131104 | tf_op jit(solution)/shard_map/ppermute | solution.py:345
  92.3 2.2 %copy-done.2 = bf16[2048,1024]{1,0:T(8,128)(2,1)S(1)} copy-done((bf16[2048,1024]{1,0:T(8,128)(2,1)S(1)}, bf16[2048,1024]{1,0:T(8,128)(2,1)}, u32[]{:S(2)}) %copy-start.2) | copy-done | bytes 4194328
  94.5 3.7 %project.1 = (bf16[2,64,1024]{2,1,0:T(8,128)(2,1)S(1)}, bf16[2,64,1024]{2,1,0:T(8,128)(2,1)S(1)}) custom-call(bf16[8,2,64,128]{3,2,1,0:T(8,128)(2,1)S(1)} %all-to-all-done.2.lent_ref, bf16[8,64,128]{2,1,0:T(8,128)(2,1)S(1)} %get-tuple-element.49.refs_0_, bf16[8,64,128]{2,1,0:T(8,128)(2,1)S(1)} %collective-permute-done.refs_1_, ...), custom_call_target="tpu_custom_call" | custom-call | tf_op jit(solution)/shard_map/project/pallas_call | solution.py:353
  98.3 1.5 %collective-permute-done.7 = bf16[2,64,1024]{2,1,0:T(8,128)(2,1)S(1)} collective-permute-done((bf16[2,64,1024]{2,1,0:T(8,128)(2,1)S(1)}, bf16[2,64,1024]{2,1,0:T(8,128)(2,1)S(1)}, u32[]{:S(2)}, u32[]{:S(2)}) %collective-permute-start.7) | collective-permute-done | bytes 262176 | tf_op jit(solution)/shard_map/ppermute | solution.py:374
  99.9 1.6 %collective-permute-start.8 = (bf16[1,64,1024]{2,1,0:T(8,128)(2,1)S(1)}, bf16[1,64,1024]{2,1,0:T(8,128)(2,1)S(1)}, u32[]{:S(2)}, u32[]{:S(2)}) collective-permute-start(bf16[1,64,1024]{2,1,0:T(8,128)(2,1)S(1)} %fusion.2), channel_id=1, source_target_pairs={{0,2},{1,3},{2,0},{3,1},{4,6},{5,7},{6,4},{7,5},{8,10},{9,11},{10,... | collective-permute-start | bytes 393224 | tf_op jit(solution)/shard_map/ppermute | solution.py:374
  101.5 4.0 %collective-permute-done.8 = bf16[1,64,1024]{2,1,0:T(8,128)(2,1)S(1)} collective-permute-done((bf16[1,64,1024]{2,1,0:T(8,128)(2,1)S(1)}, bf16[1,64,1024]{2,1,0:T(8,128)(2,1)S(1)}, u32[]{:S(2)}, u32[]{:S(2)}) %collective-permute-start.8) | collective-permute-done | bytes 131104 | tf_op jit(solution)/shard_map/ppermute | solution.py:374
  (26 shorter events, 2.7 us)
Async XLA Ops:
  2.7 48.9 %all-to-all-start.1 = ((bf16[8,80,128]{2,1,0:T(8,128)(2,1)}), bf16[8,80,128]{2,1,0:T(8,128)(2,1)S(1)}, u32[]{:S(2)}, u32[]{:S(2)}) async-start(bf16[8,80,128]{2,1,0:T(8,128)(2,1)} %ask.2), calls=%async_computation.1 | async-start | bytes 327680 | tf_op jit(solution)/shard_map/all_to_all | solution.py:286
  12.1 3.4 %copy-start = (bf16[64,256,2,128]{3,2,1,0:T(2,128)(2,1)S(1)}, bf16[64,256,2,128]{3,2,1,0:T(2,128)(2,1)}, u32[]{:S(2)}) copy-start(bf16[64,256,2,128]{3,2,1,0:T(2,128)(2,1)} %param.13) | copy-start | bytes 25165828
  15.5 0.7 copy-start.3
  16.2 0.7 copy-start.4
  16.9 35.8 %copy-start.5 = (bf16[8,4,16,128]{3,2,1,0:T(8,128)(2,1)S(1)}, bf16[8,4,16,128]{3,2,1,0:T(8,128)(2,1)}, u32[]{:S(2)}) copy-start(bf16[8,4,16,128]{3,2,1,0:T(8,128)(2,1)} %param.10) | copy-start | bytes 393220
  16.9 35.8 %copy-start.6 = (s32[64]{0:T(128)S(1)}, s32[64]{0:T(128)}, u32[]{:S(2)}) copy-start(s32[64]{0:T(128)} %slot_ref.5) | copy-start | bytes 772
  16.9 35.8 %copy-start.7 = (s32[64]{0:T(128)S(1)}, s32[64]{0:T(128)}, u32[]{:S(2)}) copy-start(s32[64]{0:T(128)} %len_ref.5) | copy-start | bytes 772
  52.8 3.4 %copy-start.1 = (bf16[64,256,2,128]{3,2,1,0:T(2,128)(2,1)S(1)}, bf16[64,256,2,128]{3,2,1,0:T(2,128)(2,1)}, u32[]{:S(2)}) copy-start(bf16[64,256,2,128]{3,2,1,0:T(2,128)(2,1)} %param.13) | copy-start | bytes 25165828
  60.8 31.5 %all-to-all-start.2 = ((bf16[8,2,64,128]{3,2,1,0:T(8,128)(2,1)}), bf16[8,2,64,128]{3,2,1,0:T(8,128)(2,1)S(1)}, u32[]{:S(2)}, u32[]{:S(2)}) async-start(bf16[8,2,64,128]{3,2,1,0:T(8,128)(2,1)} %broadcast_in_dim.19), calls=%async_computation.2 | async-start | bytes 524288 | tf_op jit(solution)/shard_map/all_to_all | solution.py:347
  65.9 12.6 %collective-permute-start.5 = (bf16[8,64,128]{2,1,0:T(8,128)(2,1)S(1)}, bf16[8,64,128]{2,1,0:T(8,128)(2,1)S(1)}, u32[]{:S(2)}, u32[]{:S(2)}) collective-permute-start(bf16[8,64,128]{2,1,0:T(8,128)(2,1)S(1)} %get-tuple-element.49.refs_0_), channel_id=1, source_target_pairs={{0,24},{4,28},{8,16},{12,20},{16,8},{20,12},{24,0},{28,4},{1,25},{... | collective-permute-start | bytes 393224 | tf_op jit(solution)/shard_map/ppermute | solution.py:345
  69.7 15.7 %collective-permute-start.3 = (bf16[8,64,128]{2,1,0:T(8,128)(2,1)S(1)}, bf16[8,64,128]{2,1,0:T(8,128)(2,1)S(1)}, u32[]{:S(2)}, u32[]{:S(2)}) collective-permute-start(bf16[8,64,128]{2,1,0:T(8,128)(2,1)S(1)} %get-tuple-element.49.refs_0_), channel_id=1, source_target_pairs={{0,16},{4,20},{8,24},{12,28},{16,0},{20,4},{24,8},{28,12},{1,17},{... | collective-permute-start | bytes 393224 | tf_op jit(solution)/shard_map/ppermute | solution.py:345
  69.7 17.2 %collective-permute-start.1 = (bf16[8,64,128]{2,1,0:T(8,128)(2,1)S(1)}, bf16[8,64,128]{2,1,0:T(8,128)(2,1)S(1)}, u32[]{:S(2)}, u32[]{:S(2)}) collective-permute-start(bf16[8,64,128]{2,1,0:T(8,128)(2,1)S(1)} %get-tuple-element.49.refs_0_), channel_id=1, source_target_pairs={{0,8},{4,12},{8,0},{12,4},{16,24},{20,28},{24,16},{28,20},{1,9},{5... | collective-permute-start | bytes 393224 | tf_op jit(solution)/shard_map/ppermute | solution.py:345
  70.3 17.2 %collective-permute-start = (bf16[8,64,128]{2,1,0:T(8,128)(2,1)S(1)}, bf16[8,64,128]{2,1,0:T(8,128)(2,1)S(1)}, u32[]{:S(2)}, u32[]{:S(2)}) collective-permute-start(bf16[8,64,128]{2,1,0:T(8,128)(2,1)S(1)} %get-tuple-element.49.refs_0_), channel_id=1, source_target_pairs={{0,4},{4,0},{8,12},{12,8},{16,20},{20,16},{24,28},{28,24},{1,5},{5... | collective-permute-start | bytes 393224 | tf_op jit(solution)/shard_map/ppermute | solution.py:345
  78.5 9.0 %collective-permute-start.6 = (bf16[8,64,128]{2,1,0:T(8,128)(2,1)S(1)}, bf16[8,64,128]{2,1,0:T(8,128)(2,1)S(1)}, u32[]{:S(2)}, u32[]{:S(2)}) collective-permute-start(bf16[8,64,128]{2,1,0:T(8,128)(2,1)S(1)} %collective-permute-done.5.refs_6_), channel_id=1, source_target_pairs={{0,4},{4,0},{8,12},{12,8},{16,20},{20,16},{24,28},{28,24},{1,5},{5... | collective-permute-start | bytes 393224 | tf_op jit(solution)/shard_map/ppermute | solution.py:345
  85.5 5.4 %collective-permute-start.4 = (bf16[8,64,128]{2,1,0:T(8,128)(2,1)S(1)}, bf16[8,64,128]{2,1,0:T(8,128)(2,1)S(1)}, u32[]{:S(2)}, u32[]{:S(2)}) collective-permute-start(bf16[8,64,128]{2,1,0:T(8,128)(2,1)S(1)} %collective-permute-done.3.refs_4_), channel_id=1, source_target_pairs={{0,4},{4,0},{8,12},{12,8},{16,20},{20,16},{24,28},{28,24},{1,5},{5... | collective-permute-start | bytes 393224 | tf_op jit(solution)/shard_map/ppermute | solution.py:345
  86.9 5.4 %collective-permute-start.2 = (bf16[8,64,128]{2,1,0:T(8,128)(2,1)S(1)}, bf16[8,64,128]{2,1,0:T(8,128)(2,1)S(1)}, u32[]{:S(2)}, u32[]{:S(2)}) collective-permute-start(bf16[8,64,128]{2,1,0:T(8,128)(2,1)S(1)} %collective-permute-done.1.refs_2_), channel_id=1, source_target_pairs={{0,4},{4,0},{8,12},{12,8},{16,20},{20,16},{24,28},{28,24},{1,5},{5... | collective-permute-start | bytes 393224 | tf_op jit(solution)/shard_map/ppermute | solution.py:345
  92.3 2.2 %copy-start.2 = (bf16[2048,1024]{1,0:T(8,128)(2,1)S(1)}, bf16[2048,1024]{1,0:T(8,128)(2,1)}, u32[]{:S(2)}) copy-start(bf16[2048,1024]{1,0:T(8,128)(2,1)} %refs_8_.1) | copy-start | bytes 12582916
  98.2 1.6 %collective-permute-start.7 = (bf16[2,64,1024]{2,1,0:T(8,128)(2,1)S(1)}, bf16[2,64,1024]{2,1,0:T(8,128)(2,1)S(1)}, u32[]{:S(2)}, u32[]{:S(2)}) collective-permute-start(bf16[2,64,1024]{2,1,0:T(8,128)(2,1)S(1)} %get-tuple-element.51), channel_id=1, source_target_pairs={{0,1},{1,0},{2,3},{3,2},{4,5},{5,4},{6,7},{7,6},{8,9},{9,8},{10,11... | collective-permute-start | bytes 786440 | tf_op jit(solution)/shard_map/ppermute | solution.py:374
  99.9 5.6 %collective-permute-start.8 = (bf16[1,64,1024]{2,1,0:T(8,128)(2,1)S(1)}, bf16[1,64,1024]{2,1,0:T(8,128)(2,1)S(1)}, u32[]{:S(2)}, u32[]{:S(2)}) collective-permute-start(bf16[1,64,1024]{2,1,0:T(8,128)(2,1)S(1)} %fusion.2), channel_id=1, source_target_pairs={{0,2},{1,3},{2,0},{3,1},{4,6},{5,7},{6,4},{7,5},{8,10},{9,11},{10,... | collective-permute-start | bytes 393224 | tf_op jit(solution)/shard_map/ppermute | solution.py:374
